TPU v7x, 32 devices: a whole 2x2x4 slice. The times are simulated.
32 devices in a mesh: fsdp: 8 (over y, x, core), seq: 4 (over z).
Axes of the slice: x: 2, y: 2, z: 4, core: 2. Of those that a mesh axis runs over, the one named last changes fastest.
Arguments:
- query_rows: bfloat16 [16, 768, 16, 128], P('fsdp', 'seq'), may hold values from -6 to 6
- key_rows: bfloat16 [16, 768, 16, 128], P('fsdp', 'seq'), may hold values from -6 to 6
- value_rows: bfloat16 [16, 768, 16, 128], P('fsdp', 'seq'), may hold values from -6 to 6
- gate_rows: bfloat16 [16, 768, 16, 128], P('fsdp', 'seq'), may hold values from -6 to 6
- out_weight: bfloat16 [2048, 2048], P('fsdp'), may hold values from -0.125 to 0.125
Outputs:
- block_out: bfloat16 [16, 768, 2048], P('fsdp', 'seq')
All inputs are finite; a program needn't handle non-finite values.
Results may differ from a plain program's by a relative error of at most 0.006.
Values may be sent and summed in bfloat16 or wider, within the bound.
A program may use at most 64 MiB of HBM per device.

v0:
```python
import functools
import math

import jax
import jax.numpy as jnp
from jax import lax
from jax.experimental import pallas as pl
from jax.experimental.pallas import tpu as pltpu
from jax.sharding import PartitionSpec as P

MESH = pl.DeviceIdType.MESH
CHUNK_HEADS = 2
HOP_LAG = 3
STAGE_EIGHTHS = 8
SECOND_EIGHTHS = 2
VMEM_MIB = 56
PIECES = 2
COLUMN_TILE = 512


def feature_map(wide):
    return (wide * wide + 0.1).astype(jnp.bfloat16)


def chip_grid(fsdp):
    chips = fsdp // 2
    along_x = max(size for size in range(1, math.isqrt(chips) + 1) if chips % size == 0)
    return chips // along_x, along_x


def kernel(
    fsdp,
    seq,
    q_hbm,
    k_hbm,
    v_hbm,
    g_hbm,
    w_hbm,
    out_hbm,
    q_raw,
    k_raw,
    v_raw,
    g_raw,
    q_wide,
    k_wide,
    v_wide,
    g_wide,
    own,
    own_mass,
    came,
    gone,
    came_mass,
    gone_mass,
    weight,
    mixed,
    total,
    result,
    load_sem,
    out_sem,
    state_send,
    state_recv,
    mass_send,
    mass_recv,
    ring_send,
    ring_recv,
    core_send,
    core_recv,
):
    batch, tokens, heads, size = q_raw.shape
    rows = w_hbm.shape[0]
    width = weight.shape[1]
    count = tokens * seq
    grid_y, grid_x = chip_grid(fsdp)
    group_heads = heads // (grid_x * grid_y)
    together = math.gcd(CHUNK_HEADS, group_heads)
    turns = heads // together
    group_turns = group_heads // together
    chunks = batch * turns
    places = sorted(
        ((i, j) for i in range(grid_x) for j in range(grid_y)), key=lambda place: (sum(place), place[1])
    )
    last_stage = grid_x + grid_y - 2

    f, z = lax.axis_index("fsdp"), lax.axis_index("seq")
    core, chip = lax.rem(f, 2), f // 2
    x, y = lax.rem(chip, grid_x), chip // grid_x

    def at(chip_y, chip_x, which):
        return (chip_y * grid_x + chip_x) * 2 + which

    right_x = at(y, lax.rem(x + 1, grid_x), core)
    right_y = at(lax.rem(y + 1, grid_y), x, core)
    other_core = at(y, x, 1 - core)

    loads = {}
    for number, (name, source, target) in enumerate(
        (("k", k_hbm, k_raw), ("v", v_hbm, v_raw), ("q", q_hbm, q_raw), ("g", g_hbm, g_raw))
    ):
        loads[name] = (source, target, number)

    def load(name, b):
        source, target, number = loads[name]
        return pltpu.make_async_copy(source.at[b], target.at[b], load_sem.at[number, b])

    own_rows = weight.at[pl.ds(pl.multiple_of(f * rows, rows), rows), :]
    load_weight = pltpu.make_async_copy(w_hbm, own_rows, load_sem.at[4, 0])
    load_weight.start()
    for b in range(batch):
        load("k", b).start()
        load("v", b).start()
    for b in range(batch):
        load("q", b).start()
        load("g", b).start()

    barrier = pltpu.get_barrier_semaphore()
    greeted = [{"fsdp": other_core}]
    if grid_x > 1:
        greeted.append({"fsdp": right_x})
    if grid_x > 2:
        greeted.append({"fsdp": at(y, lax.rem(x + grid_x - 1, grid_x), core)})
    if grid_y > 1:
        greeted.append({"fsdp": right_y})
    if grid_y > 2:
        greeted.append({"fsdp": at(lax.rem(y + grid_y - 1, grid_y), x, core)})
    for device in greeted:
        pl.semaphore_signal(barrier, inc=1, device_id=device, device_id_type=MESH)

    @pl.when(z > 0)
    def _():
        pl.semaphore_signal(barrier, inc=1, device_id={"seq": z - 1}, device_id_type=MESH)

    @pl.when(z < seq - 1)
    def _():
        pl.semaphore_signal(barrier, inc=1, device_id={"seq": z + 1}, device_id_type=MESH)

    ends = jnp.where(z > 0, 1, 0) + jnp.where(z < seq - 1, 1, 0)
    load_weight.wait()
    pl.semaphore_wait(barrier, len(greeted) + ends)

    piece_rows = rows // (2 * PIECES)

    def piece(place, color, part, which):
        i, j = place
        owner = at(lax.rem(y - j + grid_y, grid_y), lax.rem(x - i + grid_x, grid_x), which)
        start = owner * rows + (color * PIECES + part) * piece_rows
        return weight.at[pl.ds(pl.multiple_of(start, piece_rows), piece_rows), :]

    number_of = {place: number for number, place in enumerate(places)}

    def slot(place, color, part):
        return (number_of[place] * 2 + color) * PIECES + part

    def ring_copy(place, color, part, along):
        further = (place[0] + 1, place[1]) if along == "x" else (place[0], place[1] + 1)
        block, landing = piece(place, color, part, core), slot(further, color, part)
        return pltpu.make_async_remote_copy(
            src_ref=block,
            dst_ref=block,
            send_sem=ring_send.at[landing],
            recv_sem=ring_recv.at[landing],
            device_id={"fsdp": right_x if along == "x" else right_y},
            device_id_type=MESH,
        )

    def core_copy(place, color, part, which):
        block = piece(place, color, part, which)
        return pltpu.make_async_remote_copy(
            src_ref=block,
            dst_ref=block,
            send_sem=core_send.at[slot(place, color, part)],
            recv_sem=core_recv.at[slot(place, color, part)],
            device_id={"fsdp": other_core},
            device_id_type=MESH,
        )

    def onward(place, color):
        i, j = place
        ways = []
        if color == 0:
            if j == 0 and i < grid_x - 1:
                ways.append("x")
            if j < grid_y - 1:
                ways.append("y")
        else:
            if i == 0 and j < grid_y - 1:
                ways.append("y")
            if i < grid_x - 1:
                ways.append("x")
        return ways

    def came_along(place, color):
        i, j = place
        if color == 0:
            return ("y", (i, j - 1)) if j > 0 else ("x", (i - 1, j))
        return ("x", (i - 1, j)) if i > 0 else ("y", (i, j - 1))

    def stage(number, orders=(0, 1)):
        for order in orders:
            for part in range(PIECES):
                for place in places:
                    if sum(place) != number:
                        continue
                    for color in range(2):
                        if order == 0 and number > 0:
                            along, before = came_along(place, color)
                            block, landing = piece(place, color, part, core), slot(place, color, part)
                            pltpu.make_async_remote_copy(
                                src_ref=block,
                                dst_ref=block,
                                send_sem=ring_send.at[landing],
                                recv_sem=ring_recv.at[landing],
                                device_id={"fsdp": right_x},
                                device_id_type=MESH,
                            ).wait_recv()
                        ways = onward(place, color)
                        if order < len(ways):
                            ring_copy(place, color, part, ways[order]).start()
                        if order == 0:
                            core_copy(place, color, part, core).start()

    stage(0, (0,))

    leading = jnp.where(z < seq // 2, 0, 1)
    trailing = 1 - leading

    def has_in(d):
        return jnp.where(d == 0, z, seq - 1 - z) > 0

    def has_out(d):
        return jnp.where(d == 0, seq - 1 - z, z) > 0

    def state_copy(d, c):
        return pltpu.make_async_remote_copy(
            src_ref=gone.at[d, c],
            dst_ref=came.at[d, c],
            send_sem=state_send.at[d, c],
            recv_sem=state_recv.at[d, c],
            device_id={"seq": z + 1 - 2 * d},
            device_id_type=MESH,
        )

    def mass_copy(d, b):
        return pltpu.make_async_remote_copy(
            src_ref=gone_mass.at[d, b],
            dst_ref=came_mass.at[d, b],
            send_sem=mass_send.at[d, b],
            recv_sem=mass_recv.at[d, b],
            device_id={"seq": z + 1 - 2 * d},
            device_id_type=MESH,
        )

    def relay(d, c):
        b = c // turns

        @pl.when(lax.rem(c, turns) == 0)
        def _():
            @pl.when(has_in(d))
            def _():
                mass_copy(d, b).wait_recv()

            @pl.when(jnp.logical_not(has_in(d)))
            def _():
                came_mass[d, b] = jnp.zeros_like(came_mass[d, b])

            @pl.when(has_out(d))
            def _():
                gone_mass[d, b] = own_mass[b] + came_mass[d, b]
                mass_copy(d, b).start()

        @pl.when(has_in(d))
        def _():
            state_copy(d, c).wait_recv()

            @pl.when(has_out(d))
            def _():
                gone[d, c] = (own[c] + came[d, c].astype(jnp.float32)).astype(jnp.bfloat16)
                state_copy(d, c).start()

        @pl.when(jnp.logical_not(has_in(d)))
        def _():
            came[d, c] = jnp.zeros_like(came[d, c])

            @pl.when(has_out(d))
            def _():
                gone[d, c] = own[c].astype(jnp.bfloat16)
                state_copy(d, c).start()

    def group_of(o):
        i = j = 0
        for number, place in enumerate(places):
            i = jnp.where(o == number, place[0], i)
            j = jnp.where(o == number, place[1], j)
        return lax.rem(y - j + grid_y, grid_y) * grid_x + lax.rem(x - i + grid_x, grid_x)

    def head_of(c, n):
        order = lax.rem(c, turns) * together + n
        return group_of(order // group_heads) * group_heads + lax.rem(order, group_heads)

    step_tokens = 16

    def widen_kv(b):
        load("k", b).wait()
        load("v", b).wait()

        def body(n, mass):
            here = pl.ds(n * step_tokens, step_tokens)
            flat = pl.ds(pl.multiple_of(n * step_tokens * heads, step_tokens * heads), step_tokens * heads)
            feature = feature_map(k_raw[b, here].astype(jnp.float32)).astype(jnp.float32)
            k_wide[b, flat, :] = feature.reshape(step_tokens * heads, size)
            v_wide[b, flat, :] = v_raw[b, here].astype(jnp.float32).reshape(step_tokens * heads, size)
            return mass + jnp.sum(feature, axis=0)

        own_mass[b] = lax.fori_loop(0, tokens // step_tokens, body, jnp.zeros((heads, size), jnp.float32))

    def widen_qg(b):
        load("q", b).wait()
        load("g", b).wait()

        def body(n, carry):
            here = pl.ds(n * step_tokens, step_tokens)
            flat = pl.ds(pl.multiple_of(n * step_tokens * heads, step_tokens * heads), step_tokens * heads)
            q = q_raw[b, here].astype(jnp.float32)
            q_wide[b, flat, :] = (q * q + 0.1).reshape(step_tokens * heads, size)
            g = g_raw[b, here].astype(jnp.float32)
            g_wide[b, flat, :] = (count**0.5 / (1.0 + jnp.exp(-g))).reshape(step_tokens * heads, size)
            return carry

        lax.fori_loop(0, tokens // step_tokens, body, 0)

    def own_state(c, n):
        b, head = c // turns, head_of(c, n)
        feature = k_wide[b, pl.ds(head, tokens, stride=heads), :].astype(jnp.bfloat16)
        value = v_wide[b, pl.ds(head, tokens, stride=heads), :].astype(jnp.bfloat16)
        own[c, n] = lax.dot_general(
            value, feature, (((0,), (0,)), ((), ())), preferred_element_type=jnp.float32
        )

    def read(c, n):
        b, head = c // turns, head_of(c, n)
        state = own[c, n] + came[0, c, n].astype(jnp.float32) + came[1, c, n].astype(jnp.float32)
        one = pl.ds(head, 1)
        mass = own_mass[b, one] + came_mass[0, b, one] + came_mass[1, b, one]
        both = jnp.concatenate(
            [(state / count).astype(jnp.bfloat16), jnp.broadcast_to((mass / count).astype(jnp.bfloat16), state.shape)],
            axis=0,
        )
        feature = q_wide[b, pl.ds(head, tokens, stride=heads), :].astype(jnp.bfloat16)
        found = lax.dot_general(feature, both, (((1,), (1,)), ((), ())), preferred_element_type=jnp.float32)
        gate = g_wide[b, pl.ds(head, tokens, stride=heads), :]
        done = found[:, :size] / (found[:, size:] + 0.001) * gate
        columns = pl.ds(pl.multiple_of(head * size, size), size)
        mixed[pl.ds(pl.multiple_of(b * tokens, tokens), tokens), columns] = done.astype(jnp.bfloat16)

    def out_copy(n):
        columns = pl.ds(pl.multiple_of(n * COLUMN_TILE, COLUMN_TILE), COLUMN_TILE)
        return [
            pltpu.make_async_copy(
                result.at[pl.ds(b * tokens, tokens), columns], out_hbm.at[b, :, columns], out_sem.at[n, b]
            )
            for b in range(batch)
        ]

    def project(o):
        place = places[o]
        if sum(place) == last_stage and (o == 0 or sum(places[o - 1]) != last_stage):
            stage(last_stage) if last_stage > 0 else None
        for color in range(2):
            for part in range(PIECES):
                core_copy(place, color, part, 1 - core).wait_recv()
        deep = group_heads * size
        here = pl.ds(pl.multiple_of(group_of(o) * deep, deep), deep)

        def body(n, carry):
            columns = pl.ds(pl.multiple_of(n * COLUMN_TILE, COLUMN_TILE), COLUMN_TILE)
            term = jnp.dot(mixed[:, here], weight[here, columns], preferred_element_type=jnp.float32)
            if o > 0:
                term = total[:, columns] + term
            if o < len(places) - 1:
                total[:, columns] = term
            else:
                result[:, columns] = term.astype(jnp.bfloat16)
                for copy in out_copy(n):
                    copy.start()
            return carry

        lax.fori_loop(0, width // COLUMN_TILE, body, 0)

    nearer = jnp.minimum(z, seq - 1 - z)
    lead_lag = nearer * HOP_LAG
    trail_lag = (seq - 1 - nearer) * HOP_LAG

    def step(k, carry):
        late = k - trail_lag

        @pl.when(jnp.logical_and(k - lead_lag >= 0, k - lead_lag < chunks))
        def _():
            relay(leading, k - lead_lag)

        @pl.when(jnp.logical_and(late >= 0, late < chunks))
        def _():
            relay(trailing, late)

        @pl.when(k == SECOND_EIGHTHS * chunks // 8)
        def _():
            stage(0, (1,))

        for number in range(1, last_stage):
            @pl.when(k == number * STAGE_EIGHTHS * chunks // (8 * (last_stage - 1)))
            def _():
                stage(number)

        later = k + 1

        @pl.when(jnp.logical_and(later < chunks, lax.rem(later, turns) == 0))
        def _():
            widen_kv(later // turns)

        @pl.when(later < chunks)
        def _():
            for n in range(together):
                own_state(later, n)

        @pl.when(jnp.logical_and(late + 1 >= 0, jnp.logical_and(late + 1 < chunks, lax.rem(late + 1, turns) == 0)))
        def _():
            widen_qg((late + 1) // turns)

        @pl.when(jnp.logical_and(late >= 0, late < chunks))
        def _():
            for n in range(together):
                read(late, n)

        for o in range(len(places)):
            @pl.when(late == chunks - turns + group_turns * (o + 1) - 1)
            def _():
                project(o)

        return carry

    widen_kv(0)
    for n in range(together):
        own_state(0, n)
    lax.fori_loop(0, chunks + (seq - 1) * HOP_LAG, step, 0)

    for n in range(width // COLUMN_TILE):
        for copy in out_copy(n):
            copy.wait()
    for place in places:
        for color in range(2):
            for part in range(PIECES):
                core_copy(place, color, part, core).wait_send()
                for along in onward(place, color):
                    ring_copy(place, color, part, along).wait_send()
    for d in range(2):

        @pl.when(has_out(d))
        def _():
            for b in range(batch):
                mass_copy(d, b).wait_send()

            def body(c, carry):
                state_copy(d, c).wait_send()
                return carry

            lax.fori_loop(0, chunks, body, 0)


def local(fsdp, seq, query_rows, key_rows, value_rows, gate_rows, out_weight):
    batch, tokens, heads, size = query_rows.shape
    rows, width = out_weight.shape
    grid_y, grid_x = chip_grid(fsdp)
    slots = grid_x * grid_y * 2 * PIECES
    together = math.gcd(CHUNK_HEADS, heads // (grid_x * grid_y))
    chunks = batch * heads // together
    raw = pltpu.VMEM(query_rows.shape, jnp.bfloat16)
    wide = pltpu.VMEM((batch, tokens * heads, size), jnp.float32)
    dma = pltpu.SemaphoreType.DMA
    return pl.pallas_call(
        functools.partial(kernel, fsdp, seq),
        out_shape=jax.ShapeDtypeStruct((batch, tokens, width), jnp.bfloat16),
        in_specs=[pl.BlockSpec(memory_space=pl.ANY)] * 5,
        out_specs=pl.BlockSpec(memory_space=pl.ANY),
        scratch_shapes=[
            raw,
            raw,
            raw,
            raw,
            wide,
            wide,
            wide,
            wide,
            pltpu.VMEM((chunks, together, size, size), jnp.float32),
            pltpu.VMEM((batch, heads, size), jnp.float32),
            pltpu.VMEM((2, chunks, together, size, size), jnp.bfloat16),
            pltpu.VMEM((2, chunks, together, size, size), jnp.bfloat16),
            pltpu.VMEM((2, batch, heads, size), jnp.float32),
            pltpu.VMEM((2, batch, heads, size), jnp.float32),
            pltpu.VMEM((rows * fsdp, width), jnp.bfloat16),
            pltpu.VMEM((batch * tokens, heads * size), jnp.bfloat16),
            pltpu.VMEM((batch * tokens, width), jnp.float32),
            pltpu.VMEM((batch * tokens, width), jnp.bfloat16),
            dma((5, batch)),
            dma((width // COLUMN_TILE, batch)),
            dma((2, chunks)),
            dma((2, chunks)),
            dma((2, batch)),
            dma((2, batch)),
            dma((slots,)),
            dma((slots,)),
            dma((slots,)),
            dma((slots,)),
        ],
        compiler_params=pltpu.CompilerParams(
            collective_id=0, has_side_effects=True, vmem_limit_bytes=VMEM_MIB * 1024 * 1024
        ),
        name="attend",
    )(query_rows, key_rows, value_rows, gate_rows, out_weight)


def solution(mesh):
    row_spec = P("fsdp", "seq", None, None)
    return jax.shard_map(
        functools.partial(local, mesh.shape["fsdp"], mesh.shape["seq"]),
        mesh=mesh,
        in_specs=(row_spec, row_spec, row_spec, row_spec, P("fsdp", None)),
        out_specs=P("fsdp", "seq", None),
        check_vma=False,
    )
```

profile of v0, /device:TPU:0, one launch (start us, length us, event | category | flops | bytes accessed | tf_op | source)
XLA Modules:
  0.0 48.2 jit_solution(18235214209584422711)
XLA Ops:
  0.0 45.4 %attend.1 = bf16[2,192,2048]{2,1,0:T(8,128)(2,1)} custom-call(bf16[2,192,16,128]{3,2,1,0:T(8,128)(2,1)} %q_hbm.1, bf16[2,192,16,128]{3,2,1,0:T(8,128)(2,1)} %k_hbm.1, bf16[2,192,16,128]{3,2,1,0:T(8,128)(2,1)} %v_hbm.1, bf16[2,192,16,128]{3,2,1,0:T(8,128)(2,1)} %g_hbm.1, bf16[256,2048]{1,0:T(8,128)(2,1)} %w_hbm.1), custom_call_target="tpu_custom_call" | custom-call | tf_op jit(solution)/shard_map/attend/pallas_call | solution.py:477
  45.4 2.7 %copy.7 = bf16[2,192,2048]{2,1,0:T(8,128)(2,1)} copy(bf16[2,192,2048]{2,1,0:T(8,128)(2,1)} %attend.1) | data formatting | bytes 3145728
where the time goes:
time: 48.3 us; the launch traced here: 48.2 us
  Pallas kernels  45.4 us (94%)
  local copies, waits for them, and re-layouts  2.73 us (6%)
    pallas_call x1, Pallas kernels, local(): pl.pallas_call(functools.partial(kernel, fsdp, seq), out_shape=jax.ShapeD...  45.4 us
    unnamed x1, local copies, waits for them, and re-layouts  2.73 us

commit v1 on v0

--- a/solution.py
+++ b/solution.py
@@ -13,7 +13,7 @@
 HOP_LAG = 3
 STAGE_EIGHTHS = 8
 SECOND_EIGHTHS = 2
-VMEM_MIB = 56
+VMEM_MIB = 52
 PIECES = 2
 COLUMN_TILE = 512
 
@@ -36,7 +36,21 @@
     v_hbm,
     g_hbm,
     w_hbm,
-    out_hbm,
+    *rest,
+):
+    results, rest = rest[: q_hbm.shape[0]], rest[q_hbm.shape[0] :]
+    attend(fsdp, seq, q_hbm, k_hbm, v_hbm, g_hbm, w_hbm, results, *rest)
+
+
+def attend(
+    fsdp,
+    seq,
+    q_hbm,
+    k_hbm,
+    v_hbm,
+    g_hbm,
+    w_hbm,
+    results,
     q_raw,
     k_raw,
     v_raw,
@@ -54,9 +68,7 @@
     weight,
     mixed,
     total,
-    result,
     load_sem,
-    out_sem,
     state_send,
     state_recv,
     mass_send,
@@ -351,15 +363,6 @@
         columns = pl.ds(pl.multiple_of(head * size, size), size)
         mixed[pl.ds(pl.multiple_of(b * tokens, tokens), tokens), columns] = done.astype(jnp.bfloat16)
 
-    def out_copy(n):
-        columns = pl.ds(pl.multiple_of(n * COLUMN_TILE, COLUMN_TILE), COLUMN_TILE)
-        return [
-            pltpu.make_async_copy(
-                result.at[pl.ds(b * tokens, tokens), columns], out_hbm.at[b, :, columns], out_sem.at[n, b]
-            )
-            for b in range(batch)
-        ]
-
     def project(o):
         place = places[o]
         if sum(place) == last_stage and (o == 0 or sum(places[o - 1]) != last_stage):
@@ -378,9 +381,8 @@
             if o < len(places) - 1:
                 total[:, columns] = term
             else:
-                result[:, columns] = term.astype(jnp.bfloat16)
-                for copy in out_copy(n):
-                    copy.start()
+                for b in range(batch):
+                    results[b][:, columns] = term[b * tokens : (b + 1) * tokens].astype(jnp.bfloat16)
             return carry
 
         lax.fori_loop(0, width // COLUMN_TILE, body, 0)
@@ -441,9 +443,6 @@
         own_state(0, n)
     lax.fori_loop(0, chunks + (seq - 1) * HOP_LAG, step, 0)
 
-    for n in range(width // COLUMN_TILE):
-        for copy in out_copy(n):
-            copy.wait()
     for place in places:
         for color in range(2):
             for part in range(PIECES):
@@ -462,6 +461,15 @@
                 return carry
 
             lax.fori_loop(0, chunks, body, 0)
+
+
+def store(*refs):
+    *parts, out, sem = refs
+    copies = [pltpu.make_async_copy(part, out.at[b], sem.at[b]) for b, part in enumerate(parts)]
+    for copy in copies:
+        copy.start()
+    for copy in copies:
+        copy.wait()
 
 
 def local(fsdp, seq, query_rows, key_rows, value_rows, gate_rows, out_weight):
@@ -474,11 +482,11 @@
     raw = pltpu.VMEM(query_rows.shape, jnp.bfloat16)
     wide = pltpu.VMEM((batch, tokens * heads, size), jnp.float32)
     dma = pltpu.SemaphoreType.DMA
-    return pl.pallas_call(
+    parts = pl.pallas_call(
         functools.partial(kernel, fsdp, seq),
-        out_shape=jax.ShapeDtypeStruct((batch, tokens, width), jnp.bfloat16),
+        out_shape=[jax.ShapeDtypeStruct((tokens, width), jnp.bfloat16)] * batch,
         in_specs=[pl.BlockSpec(memory_space=pl.ANY)] * 5,
-        out_specs=pl.BlockSpec(memory_space=pl.ANY),
+        out_specs=[pl.BlockSpec(memory_space=pltpu.VMEM)] * batch,
         scratch_shapes=[
             raw,
             raw,
@@ -497,9 +505,7 @@
             pltpu.VMEM((rows * fsdp, width), jnp.bfloat16),
             pltpu.VMEM((batch * tokens, heads * size), jnp.bfloat16),
             pltpu.VMEM((batch * tokens, width), jnp.float32),
-            pltpu.VMEM((batch * tokens, width), jnp.bfloat16),
             dma((5, batch)),
-            dma((width // COLUMN_TILE, batch)),
             dma((2, chunks)),
             dma((2, chunks)),
             dma((2, batch)),
@@ -514,6 +520,15 @@
         ),
         name="attend",
     )(query_rows, key_rows, value_rows, gate_rows, out_weight)
+    return pl.pallas_call(
+        store,
+        out_shape=jax.ShapeDtypeStruct((batch, tokens, width), jnp.bfloat16),
+        in_specs=[pl.BlockSpec(memory_space=pl.ANY)] * batch,
+        out_specs=pl.BlockSpec(memory_space=pl.ANY),
+        scratch_shapes=[dma((batch,))],
+        compiler_params=pltpu.CompilerParams(vmem_limit_bytes=8 * 1024 * 1024),
+        name="store",
+    )(*parts)
 
 
 def solution(mesh):

time: 48.3 us -> 45.9 us (0.950)
  local copies, waits for them, and re-layouts: 2.73 us -> 0 us
    unnamed x1 -> x0, local copies, waits for them, and re-layouts: 2.73 us -> none
    pallas_call x1 -> x2, Pallas kernels: 45.4 us -> 45.7 us  [the longest x1 44.6 us: local(): pl.pallas_call(functools.partial(kernel, fsdp, seq), out_shape=[jax.Shape...]
where the time goes in v1:
time: 45.9 us; the launch traced here: 45.7 us
  Pallas kernels  45.7 us (100%)
    pallas_call x1, Pallas kernels, local(): pl.pallas_call(functools.partial(kernel, fsdp, seq), out_shape=[jax.Shape...  44.6 us
    pallas_call x1, Pallas kernels, local(): pl.pallas_call(store, out_shape=jax.ShapeDtypeStruct((batch, tokens, widt...  1.16 us

profile of v1, /device:TPU:0, one launch (start us, length us, event | category | flops | bytes accessed | tf_op | source)
XLA Modules:
  0.0 45.7 jit_solution(1557610387200344542)
XLA Ops:
  0.0 44.6 %attend.1 = (bf16[192,2048]{1,0:T(8,128)(2,1)S(1)}, bf16[192,2048]{1,0:T(8,128)(2,1)S(1)}) custom-call(bf16[2,192,16,128]{3,2,1,0:T(8,128)(2,1)} %q_hbm.1, bf16[2,192,16,128]{3,2,1,0:T(8,128)(2,1)} %k_hbm.1, bf16[2,192,16,128]{3,2,1,0:T(8,128)(2,1)} %v_hbm.1, bf16[2,192,16,128]{3,2,1,0:T(8,128)(2,1)} %g_hbm.1, bf16[256,2048]{1,0:T(8,128)(2,1)} %w_hbm.1), custom_call_target="tpu_custom_call" | custom-call | tf_op jit(solution)/shard_map/attend/pallas_call | solution.py:485
  44.6 1.2 %store.1 = bf16[2,192,2048]{2,1,0:T(8,128)(2,1)} custom-call(bf16[192,2048]{1,0:T(8,128)(2,1)S(1)} %get-tuple-element.7.refs_0_, bf16[192,2048]{1,0:T(8,128)(2,1)S(1)} %get-tuple-element.8.refs_1_), custom_call_target="tpu_custom_call" | custom-call | tf_op jit(solution)/shard_map/store/pallas_call | solution.py:523

commit v2 on v1

--- a/solution.py
+++ b/solution.py
@@ -15,7 +15,7 @@
 SECOND_EIGHTHS = 2
 VMEM_MIB = 52
 PIECES = 2
-COLUMN_TILE = 512
+COLUMN_TILE = 1024
 
 
 def feature_map(wide):

time: 45.9 us -> 45.2 us (0.985)
  Pallas kernels: 45.7 us -> 45 us
    pallas_call x1, Pallas kernels: 44.6 us -> 43.9 us  [local(): pl.pallas_call(functools.partial(kernel, fsdp, seq), out_shape=[jax.Shape...]
where the time goes in v2:
time: 45.2 us; the launch traced here: 45.1 us
  Pallas kernels  45 us (100%)
    pallas_call x1, Pallas kernels, local(): pl.pallas_call(functools.partial(kernel, fsdp, seq), out_shape=[jax.Shape...  43.9 us
    pallas_call x1, Pallas kernels, local(): pl.pallas_call(store, out_shape=jax.ShapeDtypeStruct((batch, tokens, widt...  1.16 us

profile of v2, /device:TPU:0, one launch (start us, length us, event | category | flops | bytes accessed | tf_op | source)
XLA Modules:
  0.0 45.1 jit_solution(11044063561634275586)
XLA Ops:
  0.0 43.9 %attend.1 = (bf16[192,2048]{1,0:T(8,128)(2,1)S(1)}, bf16[192,2048]{1,0:T(8,128)(2,1)S(1)}) custom-call(bf16[2,192,16,128]{3,2,1,0:T(8,128)(2,1)} %q_hbm.1, bf16[2,192,16,128]{3,2,1,0:T(8,128)(2,1)} %k_hbm.1, bf16[2,192,16,128]{3,2,1,0:T(8,128)(2,1)} %v_hbm.1, bf16[2,192,16,128]{3,2,1,0:T(8,128)(2,1)} %g_hbm.1, bf16[256,2048]{1,0:T(8,128)(2,1)} %w_hbm.1), custom_call_target="tpu_custom_call" | custom-call | tf_op jit(solution)/shard_map/attend/pallas_call | solution.py:485
  43.9 1.2 %store.1 = bf16[2,192,2048]{2,1,0:T(8,128)(2,1)} custom-call(bf16[192,2048]{1,0:T(8,128)(2,1)S(1)} %get-tuple-element.7.refs_0_, bf16[192,2048]{1,0:T(8,128)(2,1)S(1)} %get-tuple-element.8.refs_1_), custom_call_target="tpu_custom_call" | custom-call | tf_op jit(solution)/shard_map/store/pallas_call | solution.py:523

commit v3 on v2

--- a/solution.py
+++ b/solution.py
@@ -367,18 +367,29 @@
         place = places[o]
         if sum(place) == last_stage and (o == 0 or sum(places[o - 1]) != last_stage):
             stage(last_stage) if last_stage > 0 else None
+        last = o == len(places) - 1
+        if last and rows % 128 == 0 and o > 0:
+            project_part(o, group_of(o) * 2 * rows + core * rows, rows, False)
+            arrived(place)
+            project_part(o, group_of(o) * 2 * rows + (1 - core) * rows, rows, True)
+        else:
+            arrived(place)
+            project_part(o, group_of(o) * 2 * rows, 2 * rows, last)
+
+    def arrived(place):
         for color in range(2):
             for part in range(PIECES):
                 core_copy(place, color, part, 1 - core).wait_recv()
-        deep = group_heads * size
-        here = pl.ds(pl.multiple_of(group_of(o) * deep, deep), deep)
+
+    def project_part(o, start, deep, last):
+        here = pl.ds(pl.multiple_of(start, deep), deep)
 
         def body(n, carry):
             columns = pl.ds(pl.multiple_of(n * COLUMN_TILE, COLUMN_TILE), COLUMN_TILE)
             term = jnp.dot(mixed[:, here], weight[here, columns], preferred_element_type=jnp.float32)
             if o > 0:
                 term = total[:, columns] + term
-            if o < len(places) - 1:
+            if not last:
                 total[:, columns] = term
             else:
                 for b in range(batch):

time: 45.2 us -> 44.8 us (level)
  no operation moved by 1% of the time
where the time goes in v3:
time: 44.8 us; the launch traced here: 44.7 us
  Pallas kernels  44.6 us (100%)
    pallas_call x1, Pallas kernels, local(): pl.pallas_call(functools.partial(kernel, fsdp, seq), out_shape=[jax.Shape...  43.5 us
    pallas_call x1, Pallas kernels, local(): pl.pallas_call(store, out_shape=jax.ShapeDtypeStruct((batch, tokens, widt...  1.16 us

profile of v3, /device:TPU:0, one launch (start us, length us, event | category | flops | bytes accessed | tf_op | source)
XLA Modules:
  0.0 44.7 jit_solution(13840929844416363018)
XLA Ops:
  0.0 43.5 %attend.1 = (bf16[192,2048]{1,0:T(8,128)(2,1)S(1)}, bf16[192,2048]{1,0:T(8,128)(2,1)S(1)}) custom-call(bf16[2,192,16,128]{3,2,1,0:T(8,128)(2,1)} %q_hbm.1, bf16[2,192,16,128]{3,2,1,0:T(8,128)(2,1)} %k_hbm.1, bf16[2,192,16,128]{3,2,1,0:T(8,128)(2,1)} %v_hbm.1, bf16[2,192,16,128]{3,2,1,0:T(8,128)(2,1)} %g_hbm.1, bf16[256,2048]{1,0:T(8,128)(2,1)} %w_hbm.1), custom_call_target="tpu_custom_call" | custom-call | tf_op jit(solution)/shard_map/attend/pallas_call | solution.py:496
  43.5 1.2 %store.1 = bf16[2,192,2048]{2,1,0:T(8,128)(2,1)} custom-call(bf16[192,2048]{1,0:T(8,128)(2,1)S(1)} %get-tuple-element.7.refs_0_, bf16[192,2048]{1,0:T(8,128)(2,1)S(1)} %get-tuple-element.8.refs_1_), custom_call_target="tpu_custom_call" | custom-call | tf_op jit(solution)/shard_map/store/pallas_call | solution.py:534

commit v4 on v3

--- a/solution.py
+++ b/solution.py
@@ -11,11 +11,11 @@
 MESH = pl.DeviceIdType.MESH
 CHUNK_HEADS = 2
 HOP_LAG = 3
-STAGE_EIGHTHS = 8
-SECOND_EIGHTHS = 2
+STAGE_SIXTEENTHS = 16
+SECOND_SIXTEENTHS = 5
 VMEM_MIB = 52
 PIECES = 2
-COLUMN_TILE = 1024
+COLUMN_TILE = 2048
 
 
 def feature_map(wide):
@@ -120,9 +120,6 @@
     for b in range(batch):
         load("k", b).start()
         load("v", b).start()
-    for b in range(batch):
-        load("q", b).start()
-        load("g", b).start()
 
     barrier = pltpu.get_barrier_semaphore()
     greeted = [{"fsdp": other_core}]
@@ -231,6 +228,9 @@
                             core_copy(place, color, part, core).start()
 
     stage(0, (0,))
+    for b in range(batch):
+        load("q", b).start()
+        load("g", b).start()
 
     leading = jnp.where(z < seq // 2, 0, 1)
     trailing = 1 - leading
@@ -413,12 +413,12 @@
         def _():
             relay(trailing, late)
 
-        @pl.when(k == SECOND_EIGHTHS * chunks // 8)
+        @pl.when(k == SECOND_SIXTEENTHS * chunks // 16)
         def _():
             stage(0, (1,))
 
         for number in range(1, last_stage):
-            @pl.when(k == number * STAGE_EIGHTHS * chunks // (8 * (last_stage - 1)))
+            @pl.when(k == number * STAGE_SIXTEENTHS * chunks // (16 * (last_stage - 1)))
             def _():
                 stage(number)
 

time: 44.8 us -> 44.6 us (level)
  no operation moved by 1% of the time
where the time goes in v4:
time: 44.6 us; the launch traced here: 44.4 us
  Pallas kernels  44.4 us (100%)
    pallas_call x1, Pallas kernels, local(): pl.pallas_call(functools.partial(kernel, fsdp, seq), out_shape=[jax.Shape...  43.3 us
    pallas_call x1, Pallas kernels, local(): pl.pallas_call(store, out_shape=jax.ShapeDtypeStruct((batch, tokens, widt...  1.16 us

profile of v4, /device:TPU:0, one launch (start us, length us, event | category | flops | bytes accessed | tf_op | source)
XLA Modules:
  0.0 44.4 jit_solution(2623105558393445314)
XLA Ops:
  0.0 43.3 %attend.1 = (bf16[192,2048]{1,0:T(8,128)(2,1)S(1)}, bf16[192,2048]{1,0:T(8,128)(2,1)S(1)}) custom-call(bf16[2,192,16,128]{3,2,1,0:T(8,128)(2,1)} %q_hbm.1, bf16[2,192,16,128]{3,2,1,0:T(8,128)(2,1)} %k_hbm.1, bf16[2,192,16,128]{3,2,1,0:T(8,128)(2,1)} %v_hbm.1, bf16[2,192,16,128]{3,2,1,0:T(8,128)(2,1)} %g_hbm.1, bf16[256,2048]{1,0:T(8,128)(2,1)} %w_hbm.1), custom_call_target="tpu_custom_call" | custom-call | tf_op jit(solution)/shard_map/attend/pallas_call | solution.py:496
  43.3 1.2 %store.1 = bf16[2,192,2048]{2,1,0:T(8,128)(2,1)} custom-call(bf16[192,2048]{1,0:T(8,128)(2,1)S(1)} %get-tuple-element.7.refs_0_, bf16[192,2048]{1,0:T(8,128)(2,1)S(1)} %get-tuple-element.8.refs_1_), custom_call_target="tpu_custom_call" | custom-call | tf_op jit(solution)/shard_map/store/pallas_call | solution.py:534

commit v5 on v4

--- a/solution.py
+++ b/solution.py
@@ -203,9 +203,9 @@
             return ("y", (i, j - 1)) if j > 0 else ("x", (i - 1, j))
         return ("x", (i - 1, j)) if i > 0 else ("y", (i, j - 1))
 
-    def stage(number, orders=(0, 1)):
+    def stage(number, orders=(0, 1), parts=range(PIECES)):
         for order in orders:
-            for part in range(PIECES):
+            for part in parts:
                 for place in places:
                     if sum(place) != number:
                         continue
@@ -366,7 +366,7 @@
     def project(o):
         place = places[o]
         if sum(place) == last_stage and (o == 0 or sum(places[o - 1]) != last_stage):
-            stage(last_stage) if last_stage > 0 else None
+            stage(last_stage, (0,), range(1, PIECES)) if last_stage > 0 else None
         last = o == len(places) - 1
         if last and rows % 128 == 0 and o > 0:
             project_part(o, group_of(o) * 2 * rows + core * rows, rows, False)
@@ -421,6 +421,9 @@
             @pl.when(k == number * STAGE_SIXTEENTHS * chunks // (16 * (last_stage - 1)))
             def _():
                 stage(number)
+
+        if last_stage > 0:
+            pl.when(late == chunks - 1)(functools.partial(stage, last_stage, (0,), range(1)))
 
         later = k + 1
 

time: 44.6 us -> 44.3 us (level)
  no operation moved by 1% of the time
where the time goes in v5:
time: 44.3 us; the launch traced here: 44.1 us
  Pallas kernels  44.1 us (100%)
    pallas_call x1, Pallas kernels, local(): pl.pallas_call(functools.partial(kernel, fsdp, seq), out_shape=[jax.Shape...  43 us
    pallas_call x1, Pallas kernels, local(): pl.pallas_call(store, out_shape=jax.ShapeDtypeStruct((batch, tokens, widt...  1.16 us

profile of v5, /device:TPU:0, one launch (start us, length us, event | category | flops | bytes accessed | tf_op | source)
XLA Modules:
  0.0 44.1 jit_solution(2959385925866404509)
XLA Ops:
  0.0 43.0 %attend.1 = (bf16[192,2048]{1,0:T(8,128)(2,1)S(1)}, bf16[192,2048]{1,0:T(8,128)(2,1)S(1)}) custom-call(bf16[2,192,16,128]{3,2,1,0:T(8,128)(2,1)} %q_hbm.1, bf16[2,192,16,128]{3,2,1,0:T(8,128)(2,1)} %k_hbm.1, bf16[2,192,16,128]{3,2,1,0:T(8,128)(2,1)} %v_hbm.1, bf16[2,192,16,128]{3,2,1,0:T(8,128)(2,1)} %g_hbm.1, bf16[256,2048]{1,0:T(8,128)(2,1)} %w_hbm.1), custom_call_target="tpu_custom_call" | custom-call | tf_op jit(solution)/shard_map/attend/pallas_call | solution.py:499
  43.0 1.2 %store.1 = bf16[2,192,2048]{2,1,0:T(8,128)(2,1)} custom-call(bf16[192,2048]{1,0:T(8,128)(2,1)S(1)} %get-tuple-element.7.refs_0_, bf16[192,2048]{1,0:T(8,128)(2,1)S(1)} %get-tuple-element.8.refs_1_), custom_call_target="tpu_custom_call" | custom-call | tf_op jit(solution)/shard_map/store/pallas_call | solution.py:537

commit v6 on v5

--- a/solution.py
+++ b/solution.py
@@ -12,7 +12,7 @@
 CHUNK_HEADS = 2
 HOP_LAG = 3
 STAGE_SIXTEENTHS = 16
-SECOND_SIXTEENTHS = 5
+SECOND_SIXTEENTHS = 6
 VMEM_MIB = 52
 PIECES = 2
 COLUMN_TILE = 2048

time: 44.3 us -> 44.3 us (level)
  no operation moved by 1% of the time
where the time goes in v6:
time: 44.3 us; the launch traced here: 44.1 us
  Pallas kernels  44.1 us (100%)
    pallas_call x1, Pallas kernels, local(): pl.pallas_call(functools.partial(kernel, fsdp, seq), out_shape=[jax.Shape...  43 us
    pallas_call x1, Pallas kernels, local(): pl.pallas_call(store, out_shape=jax.ShapeDtypeStruct((batch, tokens, widt...  1.16 us

profile of v6, /device:TPU:0, one launch (start us, length us, event | category | flops | bytes accessed | tf_op | source)
XLA Modules:
  0.0 44.1 jit_solution(4760213002684887407)
XLA Ops:
  0.0 43.0 %attend.1 = (bf16[192,2048]{1,0:T(8,128)(2,1)S(1)}, bf16[192,2048]{1,0:T(8,128)(2,1)S(1)}) custom-call(bf16[2,192,16,128]{3,2,1,0:T(8,128)(2,1)} %q_hbm.1, bf16[2,192,16,128]{3,2,1,0:T(8,128)(2,1)} %k_hbm.1, bf16[2,192,16,128]{3,2,1,0:T(8,128)(2,1)} %v_hbm.1, bf16[2,192,16,128]{3,2,1,0:T(8,128)(2,1)} %g_hbm.1, bf16[256,2048]{1,0:T(8,128)(2,1)} %w_hbm.1), custom_call_target="tpu_custom_call" | custom-call | tf_op jit(solution)/shard_map/attend/pallas_call | solution.py:499
  43.0 1.2 %store.1 = bf16[2,192,2048]{2,1,0:T(8,128)(2,1)} custom-call(bf16[192,2048]{1,0:T(8,128)(2,1)S(1)} %get-tuple-element.7.refs_0_, bf16[192,2048]{1,0:T(8,128)(2,1)S(1)} %get-tuple-element.8.refs_1_), custom_call_target="tpu_custom_call" | custom-call | tf_op jit(solution)/shard_map/store/pallas_call | solution.py:537
